TPU v7x, 32 devices: a whole 2x2x4 slice. The times are simulated.
32 devices in a mesh: groups: 2 (over x), rows: 16 (over z, y, core).
Axes of the slice: x: 2, y: 2, z: 4, core: 2. Of those that a mesh axis runs over, the one named last changes fastest.
Arguments:
- frames: bfloat16 [16384, 2560], P(('groups', 'rows')), parts along dimension 0, may hold values from -6 to 6
- offsets: int32 [4096], P(('groups', 'rows')), parts along dimension 0, may hold values from 0 to 8173, as said below
- neighbours: int32 [32, 4096], P(None, ('groups', 'rows')), parts along dimension 1, may hold values from 0 to 2047, as said below
- initial_codes: int32 [32, 4096], P(None, ('groups', 'rows')), parts along dimension 1, may hold values from -1048576 to 1048575
- embed_weight: bfloat16 [2560, 256], replicated, may hold values from -0.125 to 0.125
- embed_bias: float32 [256], replicated, may hold values from -0.9 to 0.9
Outputs:
- affinity: float32 [32, 4096], P(None, ('groups', 'rows')), parts along dimension 1
- vectors: float32 [32, 4096], P(None, ('groups', 'rows')), parts along dimension 1
There are 2 independent parts, one for each index of `groups`. A program takes and returns all parts, laid end to end along the dimension named above; an argument that names none is the same for every part. Nothing has to cross between parts.
Inputs may be any that keep to these rules, and one draw needn't show every extreme that they name: `offsets`: the window of row i starts in the block of 512 frames numbered i // 128 and its 19 frames end before frame 8192. `neighbours`: the 32 columns of row i are distinct and differ from i; the k-th is (i + d) mod 2048 with 1 + k s <= d <= (k + 1) s, where s = 63.
All inputs are finite; a program needn't handle non-finite values.
Results may differ from a plain program's by a relative error of at most 0.012.
The roundings to bfloat16 on the way count: a program that leaves them out, or rounds other values in their place, can miss the bound.
Values may be sent and summed in bfloat16 or wider, within the bound.
No kernel may reach another device: no remote copies, remote signals or barrier semaphores. Data moves between devices by JAX's collectives and lax.ppermute only.
A program may use at most 64 MiB of HBM per device.

v0:
```python
import jax
import jax.numpy as jnp
from jax import lax
from jax.sharding import PartitionSpec as P

WIN = 19
ITERS = 3
epsilon = 1e-06
sharpness = 8.0
seed_scale = 2.0 ** (-20)


def from_behind(block, axis, distance):
    devices = range(lax.axis_size(axis))
    route = [(i - distance, i) for i in devices if i - distance in devices]
    return lax.ppermute(block, axis, route)


def block_width(length, shard_rows):
    shards = length // shard_rows
    chosen = 1
    for factor in range(1, shards + 1):
        if shards % factor == 0 and factor * shard_rows <= 4096:
            chosen = factor
    return chosen * shard_rows


def on_device(frames, offsets, neighbours, initial_codes, embed_weight, embed_bias):
    own_rows = offsets.shape[0]
    own_frames = frames.shape[0]
    kept = neighbours.shape[0]
    my_index = lax.axis_index("rows")
    next_frames = from_behind(frames[: WIN - 1], "rows", -1)
    extended = jnp.concatenate([frames, next_frames], axis=0)
    window_start = offsets - my_index * own_frames
    positions = jnp.arange(extended.shape[0], dtype=jnp.int32)[None, :]
    begins = window_start[:, None]
    window_mask = ((positions >= begins) & (positions < begins + WIN)).astype(jnp.bfloat16)
    window_sums = jnp.dot(window_mask, extended, preferred_element_type=jnp.float32)
    pooled = (window_sums * (1.0 / WIN)).astype(jnp.bfloat16)
    embedded = jnp.dot(pooled, embed_weight, preferred_element_type=jnp.float32) + embed_bias
    squares = jnp.sum(embedded * embedded, axis=1, keepdims=True)
    unit_rows = (embedded * lax.rsqrt(squares + epsilon)).astype(jnp.bfloat16)
    portion = lax.all_gather(unit_rows, "rows", axis=0, tiled=True)
    length = portion.shape[0]
    block_cols = block_width(length, own_rows)

    def one_block(block_index, carried):
        first_col = block_index * block_cols
        candidates = lax.dynamic_slice_in_dim(portion, first_col, block_cols, 0)
        scores = lax.dot_general(
            unit_rows, candidates, (((1,), (1,)), ((), ())), preferred_element_type=jnp.float32
        )
        relative = neighbours - first_col
        inside = (relative >= 0) & (relative < block_cols)
        picked = jnp.take_along_axis(scores, jnp.clip(relative, 0, block_cols - 1).T, axis=1).T
        return carried + jnp.where(inside, picked, 0.0)

    cosine = lax.fori_loop(
        0, length // block_cols, one_block, jnp.zeros((kept, own_rows), jnp.float32)
    )
    affinity = jnp.exp(sharpness * (cosine - 1.0))
    vectors = initial_codes.astype(jnp.float32) * seed_scale
    vec_count = vectors.shape[0]
    carried = vectors
    for turn_index in range(ITERS):
        gathered = lax.all_gather(carried, "rows", axis=1, tiled=True)
        if turn_index > 0:
            gram_matrix = jnp.dot(gathered, gathered.T, precision=lax.Precision.HIGHEST)
            cholesky_factor = jnp.linalg.cholesky(gram_matrix)
            gathered = jax.scipy.linalg.solve_triangular(cholesky_factor, gathered, lower=True)
        current = lax.dynamic_slice_in_dim(gathered, my_index * own_rows, own_rows, 1)
        forward = jnp.sum(affinity[None] * jnp.take(gathered, neighbours, axis=1), axis=1)
        spread = (
            jnp.zeros((vec_count, gathered.shape[1]), jnp.float32)
            .at[:, neighbours.reshape(-1)]
            .add((affinity[None] * current[:, None, :]).reshape(vec_count, -1))
        )
        mixed = 0.5 * (forward + lax.psum_scatter(spread, "rows", scatter_dimension=1, tiled=True))
        carried = mixed
    partial_gram = jnp.dot(carried, carried.T, precision=lax.Precision.HIGHEST)
    gram_matrix = lax.psum(partial_gram, "rows")
    cholesky_factor = jnp.linalg.cholesky(gram_matrix)
    carried = jax.scipy.linalg.solve_triangular(cholesky_factor, carried, lower=True)
    return (affinity, carried)


def solution(mesh):
    placed = (
        P(("groups", "rows"), None),
        P(("groups", "rows")),
        P(None, ("groups", "rows")),
        P(None, ("groups", "rows")),
        P(),
        P(),
    )
    return jax.shard_map(
        on_device,
        mesh=mesh,
        in_specs=placed,
        out_specs=(P(None, ("groups", "rows")), P(None, ("groups", "rows"))),
        check_vma=False,
    )
```

profile of v0, /device:TPU:0, one launch (start us, length us, event | category | flops | bytes accessed | tf_op | source)
XLA Modules:
  0.0 474.0 jit_solution(6266484893465082726)
XLA Ops:
  7.2 1.0 slice.17
  8.2 1.3 collective-permute-start
  9.5 0.7 broadcast_add_fusion
  10.2 1.3 collective-permute-done
  11.5 2.9 multiply_reduce_fusion
  14.3 0.7 multiply_convert_fusion
  15.4 25.2 %all_gather.13 = f32[32,2048]{1,0:T(8,128)S(1)} all-gather(f32[32,128]{1,0:T(8,128)S(1)} %convert_multiply_fusion), channel_id=1, replica_groups=mesh['groups'=2,'rows'=16] {'rows'}, dimensions={1}, use_global_device_ids=true | all-gather | bytes 278528 | tf_op jit(solution)/shard_map/all_gather | solution.py:67
  41.1 14.1 %gather_fusion.1 = f32[4096,32]{1,0:T(8,128)} fusion(f32[32,2048]{0,1:T(8,128)S(1)} %copy.50, s32[4096]{0:T(1024)S(1)} %bitcast_clamp_fusion), kind=kCustom, calls=%fused_computation.clone | custom fusion | bytes 1064960 | tf_op jit(solution)/shard_map/jit(_take)/gather | solution.py:73
  55.2 3.1 all-gather.2.cloned.1.call-done
  58.3 1.7 fusion.64
  60.0 32.8 %gather_fusion = f32[4096]{0:T(1024)S(1)} fusion(f32[128,2048]{1,0:T(8,128)S(1)} %fusion.64, s32[4096]{0:T(1024)S(1)} %reshape.113), kind=kCustom, calls=%fused_computation.3 | custom fusion | bytes 65536 | tf_op jit(solution)/shard_map/while/body/eval_jaxpr/jit(take_along_axis)/gather | solution.py:56
  93.6 23.4 %scatter_custom_fusion = f32[32,2048]{0,1:T(8,128)} fusion(s32[4096]{0:T(1024)S(1)} %bitcast.98, f32[32,4096]{0,1:T(8,128)S(1)} %bitcast_multiply_fusion.4, f32[]{:T(128)} %constant.102.clone.1), kind=kCustom, calls=%fused_computation.22 | custom fusion | flops 131072 | bytes 2359300 | tf_op jit(solution)/shard_map/scatter-add | solution.py:77
  117.1 3.2 fusion.12
  120.3 53.4 %reduce-scatter.4.cloned.1.call-done = f32[32,128]{0,1:T(8,128)} async-done(((f32[32,2048]{0,1:T(8,128)}), f32[32,128]{0,1:T(8,128)}) %reduce-scatter.4.cloned.1.call-update) | async-done | bytes 16400 | tf_op jit(solution)/shard_map/reduce_scatter | solution.py:79
  173.7 0.8 add_multiply_fusion.2
  174.6 22.6 %all_gather.14 = f32[32,2048]{0,1:T(8,128)S(1)} all-gather(f32[32,128]{0,1:T(8,128)S(1)} %add_multiply_fusion.2), channel_id=1, replica_groups=mesh['groups'=2,'rows'=16] {'rows'}, dimensions={1}, use_global_device_ids=true | all-gather | bytes 278528 | tf_op jit(solution)/shard_map/all_gather | solution.py:67
  197.1 1.8 fusion.65
  199.0 2.9 cholesky.59
  202.0 0.6 compare_reduce_fusion.2
  202.6 0.7 fusion.40
  203.3 2.4 custom-call.13
  205.7 1.2 fusion.48
  207.0 0.7 copy-done.2
  208.4 23.4 %scatter_custom_fusion.1 = f32[32,2048]{0,1:T(8,128)} fusion(s32[4096]{0:T(1024)S(1)} %bitcast.99, f32[32,4096]{0,1:T(8,128)S(1)} %bitcast_multiply_fusion.2, f32[]{:T(128)} %constant.102.clone.1), kind=kCustom, calls=%fused_computation.17 | custom fusion | flops 131072 | bytes 2359300 | tf_op jit(solution)/shard_map/scatter-add | solution.py:77
  232.0 1.3 copy.54
  233.3 14.1 %gather_fusion.2 = f32[4096,32]{1,0:T(8,128)} fusion(f32[32,2048]{0,1:T(8,128)S(1)} %copy.54, s32[4096]{0:T(1024)S(1)} %bitcast_clamp_fusion), kind=kCustom, calls=%fused_computation.1.clone | custom fusion | bytes 1064960 | tf_op jit(solution)/shard_map/jit(_take)/gather | solution.py:73
  247.4 3.2 fusion.9
  250.6 36.3 %reduce-scatter.6.cloned.1.call-done = f32[32,128]{0,1:T(8,128)} async-done(((f32[32,2048]{0,1:T(8,128)}), f32[32,128]{0,1:T(8,128)}) %reduce-scatter.6.cloned.1.call-update) | async-done | bytes 16400 | tf_op jit(solution)/shard_map/reduce_scatter | solution.py:79
  286.9 0.8 add_multiply_fusion.1
  287.8 22.6 %all_gather.15 = f32[32,2048]{0,1:T(8,128)S(1)} all-gather(f32[32,128]{0,1:T(8,128)S(1)} %add_multiply_fusion.1), channel_id=1, replica_groups=mesh['groups'=2,'rows'=16] {'rows'}, dimensions={1}, use_global_device_ids=true | all-gather | bytes 278528 | tf_op jit(solution)/shard_map/all_gather | solution.py:67
  310.3 1.8 fusion.66
  312.2 2.9 cholesky.70
  315.8 0.7 fusion.41
  316.5 2.4 custom-call.14
  318.9 1.2 fusion.45
  320.2 0.7 copy-done.1
  321.6 23.4 %scatter_custom_fusion.2 = f32[32,2048]{0,1:T(8,128)} fusion(s32[4096]{0:T(1024)S(1)} %bitcast.100, f32[32,4096]{0,1:T(8,128)S(1)} %bitcast_multiply_fusion, f32[]{:T(128)} %constant.102.clone.1), kind=kCustom, calls=%fused_computation.12 | custom fusion | flops 131072 | bytes 2359300 | tf_op jit(solution)/shard_map/scatter-add | solution.py:77
  345.0 1.3 copy.57
  346.3 14.1 %gather_fusion.3 = f32[4096,32]{1,0:T(8,128)} fusion(f32[32,2048]{0,1:T(8,128)S(1)} %copy.57, s32[4096]{0:T(1024)S(1)} %bitcast_clamp_fusion), kind=kCustom, calls=%fused_computation.2.clone | custom fusion | bytes 1064960 | tf_op jit(solution)/shard_map/jit(_take)/gather | solution.py:73
  360.4 3.2 fusion.6
  363.6 36.6 %reduce-scatter.8.cloned.1.call-done = f32[32,128]{0,1:T(8,128)} async-done(((f32[32,2048]{0,1:T(8,128)}), f32[32,128]{0,1:T(8,128)}) %reduce-scatter.8.cloned.1.call-update) | async-done | bytes 16400 | tf_op jit(solution)/shard_map/reduce_scatter | solution.py:79
  400.2 1.2 fusion.39
  401.3 57.6 %psum.7 = f32[32,32]{0,1:T(8,128)S(1)} all-reduce(f32[32,32]{0,1:T(8,128)S(1)} %fusion.39), channel_id=1, replica_groups=mesh['groups'=2,'rows'=16] {'rows'}, use_global_device_ids=true, to_apply=%region_12.16 | all-reduce | flops 1024 | bytes 8192 | tf_op jit(solution)/shard_map/psum | solution.py:82
  459.0 2.9 cholesky.81
  462.0 0.6 compare_reduce_fusion
  462.6 0.7 fusion.42
  463.3 2.4 custom-call.9
  465.7 1.7 fusion.38
  (51 shorter events, 4.3 us)
Async XLA Ops:
  7.2 4.3 copy-start
  7.2 51.1 %all-gather.2.cloned.1.call-start = ((), (), s32[]{:S(2)}) async-start(), calls=%async_computation.3 | async-start | bytes 1114112 | tf_op jit(solution)/shard_map/all_gather | solution.py:44
  8.2 3.2 collective-permute-start
  11.5 3.7 copy-start.5
  11.5 3.9 copy-start.6
  15.1 158.6 %reduce-scatter.4.cloned.1.call-start = ((), (), s32[]{:S(2)}) async-start(), calls=%async_computation.4 | async-start | bytes 1114112 | tf_op jit(solution)/shard_map/reduce_scatter | solution.py:79
  41.0 17.3 %copy-start.4 = (bf16[128,256]{1,0:T(8,128)(2,1)S(1)}, bf16[128,256]{1,0:T(8,128)(2,1)}, u32[]{:S(2)}) copy-start(bf16[128,256]{1,0:T(8,128)(2,1)} %multiply_convert_fusion) | copy-start | bytes 196612
  93.0 267.4 %copy-start.3 = (f32[32,128]{1,0:T(8,128)}, f32[32,128]{1,0:T(8,128)S(1)}, u32[]{:S(2)}) copy-start(f32[32,128]{1,0:T(8,128)S(1)} %copy.61) | copy-start | bytes 49156
  117.0 169.9 %reduce-scatter.6.cloned.1.call-start = ((), (), s32[]{:S(2)}) async-start(), calls=%async_computation.5 | async-start | bytes 1114112 | tf_op jit(solution)/shard_map/reduce_scatter | solution.py:79
  206.9 0.7 copy-start.2
  231.8 168.4 %reduce-scatter.8.cloned.1.call-start = ((), (), s32[]{:S(2)}) async-start(), calls=%async_computation.6 | async-start | bytes 1114112 | tf_op jit(solution)/shard_map/reduce_scatter | solution.py:79
  320.2 0.7 copy-start.1
Sparse Core Ops, SparseCore 0:
  15.2 43.0 all-gather.1
  117.1 56.5 reduce-scatter.3
  231.9 54.9 reduce-scatter.5
  345.1 55.0 reduce-scatter.7
where the time goes:
time: 475 us; the launch traced here: 474 us
  waiting for transfers between devices  131 us (28%)
  blocking collectives  128 us (27%)
  other arithmetic  105 us (22%)
  local copies, waits for them, and re-layouts  81.2 us (17%)
  between operations  14 us (3%)
  matrix products  13.5 us (3%)
    reduce_scatter x3, waiting for transfers between devices, on_device(): lax.psum_scatter(spread, 'rows', scatter_dimension=1, tiled=True)  126 us
    all_gather x3, blocking collectives, on_device(): gathered = lax.all_gather(carried, 'rows', axis=1, tiled=True)  70.3 us
    scatter-add x3, other arithmetic, on_device(): spread = jnp.zeros((vec_count, gathered.shape[1]), jnp.float32).at[:, nei...  70.2 us
    psum x1, blocking collectives, on_device(): gram_matrix = lax.psum(partial_gram, 'rows')  57.6 us
    gather x3, local copies, waits for them, and re-layouts, on_device(): jnp.take(gathered, neighbours, axis=1)  42.3 us
    gather x3, local copies, waits for them, and re-layouts, one_block(): jnp.take_along_axis(scores, jnp.clip(relative, 0, block_cols - 1).T, axis=1)  32.9 us
    another operation x9, other arithmetic, on_device(): cholesky_factor = jnp.linalg.cholesky(gram_matrix)  10.8 us
    reduce_sum x3, other arithmetic, on_device(): jnp.sum(affinity[None] * jnp.take(gathered, neighbours, axis=1), axis=1)  9.57 us
  transfers between devices with their start and end apart: 5, of which 5 were waited for; matrix products, arithmetic and copies ran while one was open for 12% of the time, Pallas kernels for 0%

commit v1 on v0

--- a/solution.py
+++ b/solution.py
@@ -8,6 +8,10 @@
 epsilon = 1e-06
 sharpness = 8.0
 seed_scale = 2.0 ** (-20)
+
+
+def step_on_surface_on_mesh(xs):
+    return jnp.concatenate(lax.all_gather(xs, "rows"), 1)
 
 
 def from_behind(block, axis, distance):
@@ -64,7 +68,7 @@
     vec_count = vectors.shape[0]
     carried = vectors
     for turn_index in range(ITERS):
-        gathered = lax.all_gather(carried, "rows", axis=1, tiled=True)
+        gathered = step_on_surface_on_mesh(carried)
         if turn_index > 0:
             gram_matrix = jnp.dot(gathered, gathered.T, precision=lax.Precision.HIGHEST)
             cholesky_factor = jnp.linalg.cholesky(gram_matrix)

time: 475 us -> 466 us (0.981)
  local copies, waits for them, and re-layouts: 81.2 us -> 88 us
  waiting for transfers between devices: 131 us -> 125 us
  blocking collectives: 128 us -> 123 us
  matrix products: 13.5 us -> 8.63 us
    scatter-add x0 -> x3, local copies, waits for them, and re-layouts: none -> 6.77 us  [on_device(): spread = jnp.zeros((vec_count, gathered.shape[1]), jnp.float32).at[:, nei...]
    reduce_scatter x3, waiting for transfers between devices: 126 us -> 121 us  [on_device(): lax.psum_scatter(spread, 'rows', scatter_dimension=1, tiled=True)]
where the time goes in v1:
time: 466 us; the launch traced here: 465 us
  waiting for transfers between devices  125 us (27%)
  blocking collectives  123 us (26%)
  other arithmetic  105 us (23%)
  local copies, waits for them, and re-layouts  88 us (19%)
  between operations  14 us (3%)
  matrix products  8.63 us (2%)
    reduce_scatter x3, waiting for transfers between devices, on_device(): lax.psum_scatter(spread, 'rows', scatter_dimension=1, tiled=True)  121 us
    scatter-add x3, other arithmetic, on_device(): spread = jnp.zeros((vec_count, gathered.shape[1]), jnp.float32).at[:, nei...  70.2 us
    all_gather x3, blocking collectives, step_on_surface_on_mesh(): return jnp.concatenate(lax.all_gather(xs, 'rows'), 1)  65.7 us
    psum x1, blocking collectives, on_device(): gram_matrix = lax.psum(partial_gram, 'rows')  57.6 us
    gather x3, local copies, waits for them, and re-layouts, on_device(): jnp.take(gathered, neighbours, axis=1)  42.3 us
    gather x3, local copies, waits for them, and re-layouts, one_block(): jnp.take_along_axis(scores, jnp.clip(relative, 0, block_cols - 1).T, axis=1)  32.9 us
    another operation x9, other arithmetic, on_device(): cholesky_factor = jnp.linalg.cholesky(gram_matrix)  10.8 us
    reduce_sum x3, other arithmetic, on_device(): jnp.sum(affinity[None] * jnp.take(gathered, neighbours, axis=1), axis=1)  9.57 us
  transfers between devices with their start and end apart: 5, of which 5 were waited for; matrix products, arithmetic and copies ran while one was open for 12% of the time, Pallas kernels for 0%

profile of v1, /device:TPU:0, one launch (start us, length us, event | category | flops | bytes accessed | tf_op | source)
XLA Modules:
  0.0 465.1 jit_solution(18267725946760163365)
XLA Ops:
  7.2 1.0 slice.17
  8.2 1.3 collective-permute-start
  9.5 0.7 broadcast_add_fusion
  10.2 1.3 collective-permute-done
  11.5 2.9 multiply_reduce_fusion
  14.3 0.7 multiply_convert_fusion
  15.4 25.2 %all-gather = f32[512,128]{1,0:T(8,128)S(1)} all-gather(f32[32,128]{1,0:T(8,128)S(1)} %convert_multiply_fusion), channel_id=2, replica_groups=mesh['groups'=2,'rows'=16] {'rows'}, dimensions={0}, use_global_device_ids=true | all-gather | bytes 278528 | tf_op jit(solution)/shard_map/all_gather | solution.py:14
  40.9 14.1 %gather_fusion.1 = f32[4096,32]{1,0:T(8,128)} fusion(f32[32,2048]{0,1:T(8,128)S(1)} %bitcast.111, s32[4096]{0:T(1024)S(1)} %bitcast_clamp_fusion), kind=kCustom, calls=%fused_computation.clone | custom fusion | bytes 1064960 | tf_op jit(solution)/shard_map/jit(_take)/gather | solution.py:77
  55.1 3.2 all-gather.5.cloned.1.call-done
  58.3 1.7 fusion.68
  60.0 32.8 %gather_fusion = f32[4096]{0:T(1024)S(1)} fusion(f32[128,2048]{1,0:T(8,128)S(1)} %fusion.68, s32[4096]{0:T(1024)S(1)} %reshape.137), kind=kCustom, calls=%fused_computation.3 | custom fusion | bytes 65536 | tf_op jit(solution)/shard_map/while/body/eval_jaxpr/jit(take_along_axis)/gather | solution.py:60
  93.6 23.4 %scatter_custom_fusion = f32[32,2048]{0,1:T(8,128)} fusion(s32[4096]{0:T(1024)S(1)} %bitcast.125, f32[32,4096]{0,1:T(8,128)S(1)} %bitcast_multiply_fusion.4, f32[]{:T(128)} %constant.102.clone.1), kind=kCustom, calls=%fused_computation.22 | custom fusion | flops 131072 | bytes 2359300 | tf_op jit(solution)/shard_map/scatter-add | solution.py:81
  117.0 2.3 copy.101
  119.3 3.2 fusion.12
  122.6 51.5 %reduce-scatter.4.cloned.1.call-done = f32[32,128]{1,0:T(8,128)} async-done(((f32[32,2048]{1,0:T(8,128)}), f32[32,128]{1,0:T(8,128)}) %reduce-scatter.4.cloned.1.call-update) | async-done | bytes 16400 | tf_op jit(solution)/shard_map/reduce_scatter | solution.py:83
  174.1 0.7 add_multiply_fusion.2
  174.9 20.1 %all-gather.1 = f32[512,128]{1,0:T(8,128)S(1)} all-gather(f32[32,128]{1,0:T(8,128)S(1)} %add_multiply_fusion.2), channel_id=3, replica_groups=mesh['groups'=2,'rows'=16] {'rows'}, dimensions={0}, use_global_device_ids=true | all-gather | bytes 278528 | tf_op jit(solution)/shard_map/all_gather | solution.py:14
  195.4 2.9 cholesky.59
  198.4 0.6 compare_reduce_fusion.2
  199.0 0.7 fusion.44
  199.7 2.4 custom-call.13
  202.6 0.7 copy-done.2
  204.0 23.4 %scatter_custom_fusion.1 = f32[32,2048]{0,1:T(8,128)} fusion(s32[4096]{0:T(1024)S(1)} %bitcast.126, f32[32,4096]{0,1:T(8,128)S(1)} %bitcast_multiply_fusion.2, f32[]{:T(128)} %constant.102.clone.1), kind=kCustom, calls=%fused_computation.17 | custom fusion | flops 131072 | bytes 2359300 | tf_op jit(solution)/shard_map/scatter-add | solution.py:81
  227.4 2.3 copy.107
  229.8 1.3 copy.105
  231.0 14.1 %gather_fusion.2 = f32[4096,32]{1,0:T(8,128)} fusion(f32[32,2048]{0,1:T(8,128)S(1)} %copy.105, s32[4096]{0:T(1024)S(1)} %bitcast_clamp_fusion), kind=kCustom, calls=%fused_computation.1.clone | custom fusion | bytes 1064960 | tf_op jit(solution)/shard_map/jit(_take)/gather | solution.py:77
  245.1 3.2 fusion.9
  248.4 34.5 %reduce-scatter.6.cloned.1.call-done = f32[32,128]{1,0:T(8,128)} async-done(((f32[32,2048]{1,0:T(8,128)}), f32[32,128]{1,0:T(8,128)}) %reduce-scatter.6.cloned.1.call-update) | async-done | bytes 16400 | tf_op jit(solution)/shard_map/reduce_scatter | solution.py:83
  282.8 0.7 add_multiply_fusion.1
  283.6 20.3 %all-gather.2 = f32[512,128]{1,0:T(8,128)S(1)} all-gather(f32[32,128]{1,0:T(8,128)S(1)} %add_multiply_fusion.1), channel_id=4, replica_groups=mesh['groups'=2,'rows'=16] {'rows'}, dimensions={0}, use_global_device_ids=true | all-gather | bytes 278528 | tf_op jit(solution)/shard_map/all_gather | solution.py:14
  304.3 2.9 cholesky.70
  307.3 0.6 compare_reduce_fusion.1
  307.9 0.7 fusion.45
  308.6 2.4 custom-call.14
  311.5 0.7 copy-done.1
  312.9 23.4 %scatter_custom_fusion.2 = f32[32,2048]{0,1:T(8,128)} fusion(s32[4096]{0:T(1024)S(1)} %bitcast.127, f32[32,4096]{0,1:T(8,128)S(1)} %bitcast_multiply_fusion, f32[]{:T(128)} %constant.102.clone.1), kind=kCustom, calls=%fused_computation.12 | custom fusion | flops 131072 | bytes 2359300 | tf_op jit(solution)/shard_map/scatter-add | solution.py:81
  336.3 2.3 copy.113
  338.6 1.3 copy.111
  339.9 14.1 %gather_fusion.3 = f32[4096,32]{1,0:T(8,128)} fusion(f32[32,2048]{0,1:T(8,128)S(1)} %copy.111, s32[4096]{0:T(1024)S(1)} %bitcast_clamp_fusion), kind=kCustom, calls=%fused_computation.2.clone | custom fusion | bytes 1064960 | tf_op jit(solution)/shard_map/jit(_take)/gather | solution.py:77
  353.9 3.2 fusion.6
  357.2 34.5 %reduce-scatter.8.cloned.1.call-done = f32[32,128]{1,0:T(8,128)} async-done(((f32[32,2048]{1,0:T(8,128)}), f32[32,128]{1,0:T(8,128)}) %reduce-scatter.8.cloned.1.call-update) | async-done | bytes 16400 | tf_op jit(solution)/shard_map/reduce_scatter | solution.py:83
  391.7 0.9 fusion.58
  392.7 57.6 %psum.7 = f32[32,32]{0,1:T(8,128)S(1)} all-reduce(f32[32,32]{0,1:T(8,128)S(1)} %fusion.58), channel_id=1, replica_groups=mesh['groups'=2,'rows'=16] {'rows'}, use_global_device_ids=true, to_apply=%region_12.16 | all-reduce | flops 1024 | bytes 8192 | tf_op jit(solution)/shard_map/psum | solution.py:86
  450.3 2.9 cholesky.81
  453.3 0.6 compare_reduce_fusion
  453.9 0.7 fusion.46
  454.6 2.4 custom-call.9
  457.0 1.6 fusion.47
  (56 shorter events, 5.1 us)
Async XLA Ops:
  7.2 4.3 copy-start
  7.2 51.1 %all-gather.5.cloned.1.call-start = ((), (), s32[]{:S(2)}) async-start(), calls=%async_computation.3 | async-start | bytes 1114112 | tf_op jit(solution)/shard_map/all_gather | solution.py:48
  8.2 3.2 collective-permute-start
  11.5 3.7 copy-start.5
  11.5 3.9 copy-start.6
  15.1 159.1 %reduce-scatter.4.cloned.1.call-start = ((), (), s32[]{:S(2)}) async-start(), calls=%async_computation.4 | async-start | bytes 278528 | tf_op jit(solution)/shard_map/reduce_scatter | solution.py:83
  40.9 17.4 %copy-start.4 = (bf16[128,256]{1,0:T(8,128)(2,1)S(1)}, bf16[128,256]{1,0:T(8,128)(2,1)}, u32[]{:S(2)}) copy-start(bf16[128,256]{1,0:T(8,128)(2,1)} %multiply_convert_fusion) | copy-start | bytes 196612
  93.0 261.0 %copy-start.3 = (f32[32,128]{1,0:T(8,128)}, f32[32,128]{1,0:T(8,128)S(1)}, u32[]{:S(2)}) copy-start(f32[32,128]{1,0:T(8,128)S(1)} %copy.117) | copy-start | bytes 49156
  119.3 163.6 %reduce-scatter.6.cloned.1.call-start = ((), (), s32[]{:S(2)}) async-start(), calls=%async_computation.5 | async-start | bytes 278528 | tf_op jit(solution)/shard_map/reduce_scatter | solution.py:83
  202.6 0.7 copy-start.2
  229.7 162.0 %reduce-scatter.8.cloned.1.call-start = ((), (), s32[]{:S(2)}) async-start(), calls=%async_computation.6 | async-start | bytes 278528 | tf_op jit(solution)/shard_map/reduce_scatter | solution.py:83
  311.5 0.7 copy-start.1
Sparse Core Ops, SparseCore 0:
  15.2 43.0 all-gather.4
  119.4 54.6 reduce-scatter.3
  229.8 52.9 reduce-scatter.5
  338.7 52.9 reduce-scatter.7
